TPU v7x, 32 devices: a whole 2x2x4 slice. The times are simulated.
32 devices in a mesh: seq: 8 (over z, y), head: 4 (over x, core).
Axes of the slice: x: 2, y: 2, z: 4, core: 2. Of those that a mesh axis runs over, the one named last changes fastest.
Arguments:
- query: bfloat16 [128, 32, 128], P(None, 'head'), may hold values from -8 to 8
- key_cache: bfloat16 [16384, 16, 128], P('seq', 'head'), may hold values from -6 to 6
- value_cache: bfloat16 [16384, 16, 128], P('seq', 'head'), may hold values from -6 to 6
- lengths: int32 [8], P('seq'), may hold values from 1 to 2048, 12288 in all
- out_weight: bfloat16 [4608, 4096], P('seq', 'head'), may hold values from -10 to 10
- norm_gain: float32 [4608], P('seq'), may hold values from 0.1 to 1.9
Outputs:
- normed: bfloat16 [128, 4608], P(None, 'seq')
Inputs may be any that keep to these rules, and one draw needn't show every extreme that they name: `lengths`: every block has at least one valid position, and some block is valid throughout.
All inputs are finite; a program needn't handle non-finite values.
Results may differ from a plain program's by a relative error of at most 0.0083.
Values may be sent and summed in bfloat16 or wider, within the bound.
A program may use at most 128 MiB of HBM per device.

v0:
```python
import jax
import jax.numpy as jnp
from jax import lax
from jax.sharding import PartitionSpec as P

D = 4608
QPRE = 144


def merged(value, axis, join):
    pieces = jax.tree.map(lambda part: lax.all_gather(part, axis), value)
    head = jax.tree.map(lambda part: part[0], pieces)
    tail = jax.tree.map(lambda part: part[1:], pieces)
    so_far, _ = lax.scan(lambda so_far, share: (join(so_far, share), None), head, tail)
    return so_far


def combine_partials(former, latter):
    max_former, sum_former, acc_former = former
    max_latter, sum_latter, acc_latter = latter
    new_max = jnp.maximum(max_former, max_latter)
    factor_former = jnp.exp(max_former - new_max)
    factor_latter = jnp.exp(max_latter - new_max)
    new_sum = factor_former * sum_former + factor_latter * sum_latter
    new_acc = factor_former[..., None] * acc_former + factor_latter[..., None] * acc_latter
    return (new_max, new_sum, new_acc)


def body(query, key_cache, value_cache, lengths, out_weight, norm_gain):
    tok_count, heads_local, head_dim = query.shape
    key_count, kv_local, unused_dim = key_cache.shape
    group_size = heads_local // kv_local
    score_scale = float(QPRE) ** (-0.5)
    grouped = query.reshape(tok_count, kv_local, group_size, head_dim)
    scores = (
        jnp.einsum("tkgd,ckd->kgtc", grouped, key_cache, preferred_element_type=jnp.float32)
        * score_scale
    )
    inside = lax.iota(jnp.int32, key_count) < lengths[0]
    scores = jnp.where(inside, scores, jnp.float32(-1e30))
    block_max = jnp.max(scores, axis=-1)
    weights = jnp.where(inside, jnp.exp(scores - block_max[..., None]), jnp.float32(0.0))
    block_sum = jnp.sum(weights, axis=-1)
    weights_low = weights.astype(jnp.bfloat16)
    weighted = jnp.einsum(
        "kgtc,ckd->tkgd", weights_low, value_cache, preferred_element_type=jnp.float32
    )
    weighted = weighted.reshape(tok_count, heads_local, head_dim)
    block_max = jnp.transpose(block_max, (2, 0, 1)).reshape(tok_count, heads_local)
    block_sum = jnp.transpose(block_sum, (2, 0, 1)).reshape(tok_count, heads_local)
    peak_all, total_all, combined = merged(
        (block_max, block_sum, weighted), "seq", combine_partials
    )
    attention = (
        (combined / total_all[..., None])
        .reshape(tok_count, heads_local * head_dim)
        .astype(jnp.bfloat16)
    )
    projected_part = lax.dot_general(
        attention, out_weight, (((1,), (1,)), ((), ())), preferred_element_type=jnp.float32
    )
    projected = lax.psum(projected_part, "head")
    square_part = jnp.sum(projected * projected, axis=-1)
    square_total = lax.psum(square_part, "seq")
    mean_square = square_total / D
    normed = projected * lax.rsqrt(mean_square + 1e-06)[:, None] * norm_gain[None, :]
    return normed.astype(jnp.bfloat16)


def solution(mesh):
    placed = (
        P(None, "head", None),
        P("seq", "head", None),
        P("seq", "head", None),
        P("seq"),
        P("seq", "head"),
        P("seq"),
    )
    return jax.shard_map(
        body, mesh=mesh, in_specs=placed, out_specs=P(None, "seq"), check_vma=False
    )
```

profile of v0, /device:TPU:0, one launch (start us, length us, event | category | flops | bytes accessed | tf_op | source)
XLA Modules:
  0.0 174.1 jit_solution(1487944032741304655)
XLA Ops:
  6.5 0.0 copy-start
  6.5 0.0 all-gather.2.cloned.1.call-start
  7.4 3.9 %bitcast_reduce_fusion = (f32[4,2,128]{2,1,0:T(2,128)S(1)}, f32[4,2048,128,2]{2,1,3,0:T(8,128)S(1)}) fusion(pred[2048]{0:T(1024)(128)(4,1)S(1)} %iota_compare_fusion, bf16[128,4,2,128]{3,2,1,0:T(2,128)(2,1)} %bitcast.62, bf16[2048,4,128,1]{2,1,0,3:T(4,128)(2,1)} %bitcast.61), kind=kOutput, calls=%fused_computation.9 | convolution fusion | flops 543161344 | bytes 10754048 | tf_op jit(solution)/shard_map/tkgd,ckd->kgtc/dot_general | solution.py:36
  11.2 0.0 copy-done
  11.2 0.0 copy-start.1
  11.2 3.4 %fusion.7 = f32[4,2,128,128]{3,2,1,0:T(8,128)S(1)} fusion(f32[4,2048,128,2]{2,1,3,0:T(8,128)S(1)} %get-tuple-element.64, f32[4,2,128]{2,1,0:T(2,128)S(1)} %get-tuple-element.63, pred[2048]{0:T(1024)(128)(4,1)S(1)} %iota_compare_fusion, bf16[2048,4,128,1]{2,1,0,3:T(4,128)(2,1)S(1)} %bitcast.56), kind=kOutput, calls=%fused_computation.15 | convolution fusion | flops 547356672 | bytes 11016192 | tf_op jit(solution)/shard_map/kgtc,ckd->tkgd/dot_general | solution.py:45
  14.7 0.0 copy-done.1
  14.7 1.1 copy.21
  15.8 0.0 all-gather.2.cloned.1.call-update
  15.9 0.0 all-reduce.2.cloned.1.call-start
  15.9 4.6 %fusion.6 = f32[4,2,128]{2,1,0:T(2,128)S(1)} fusion(f32[4,2048,128,2]{2,1,3,0:T(8,128)} %copy-done.1, f32[4,2,128]{2,1,0:T(2,128)S(1)} %get-tuple-element.63, pred[2048]{0:T(1024)(128)(4,1)S(1)} %iota_compare_fusion), kind=kLoop, calls=%fused_computation.14 | loop fusion | flops 10484736 | bytes 8398848 | tf_op jit(solution)/shard_map/reduce_sum | solution.py:43
  20.5 33.0 %all_gather.10 = f32[8,128,8]{1,2,0:T(8,128)S(1)} all-gather(f32[1,128,8]{1,2,0:T(8,128)S(1)} %bitcast.60), channel_id=1, replica_groups=mesh['seq'=8,'head'=4] {'seq'}, dimensions={0}, use_global_device_ids=true | all-gather | bytes 36864 | tf_op jit(solution)/shard_map/all_gather | solution.py:11
  53.5 31.8 %all_gather.9 = f32[8,128,8]{1,2,0:T(8,128)S(1)} all-gather(f32[1,128,8]{1,2,0:T(8,128)S(1)} %bitcast.59), channel_id=1, replica_groups=mesh['seq'=8,'head'=4] {'seq'}, dimensions={0}, use_global_device_ids=true | all-gather | bytes 36864 | tf_op jit(solution)/shard_map/all_gather | solution.py:11
  85.3 6.9 %all-gather.2.cloned.1.call-done = f32[8,128,8,128]{3,2,1,0:T(8,128)} async-done(((f32[1,128,8,128]{3,2,1,0:T(8,128)}), f32[8,128,8,128]{3,2,1,0:T(8,128)}) %all-gather.2.cloned.1.call-update) | async-done | bytes 4194320 | tf_op jit(solution)/shard_map/all_gather | solution.py:11
  92.2 1.1 slice_bitcast_fusion
  93.3 0.0 copy-start.2
  93.3 4.1 %slice.29 = f32[7,128,8,128]{3,2,1,0:T(8,128)} slice(f32[8,128,8,128]{3,2,1,0:T(8,128)} %all-gather.2.cloned.1.call-done), slice={[1:8], [0:128], [0:8], [0:128]} | slice | bytes 7340032 | tf_op jit(solution)/shard_map/slice | solution.py:13
  97.4 11.7 %while.14 = (s32[]{:T(128)}, f32[128,8]{0,1:T(8,128)S(1)}, f32[128,8]{0,1:T(8,128)S(1)}, f32[128,8,128]{2,1,0:T(8,128)S(1)}, f32[7,128,8]{1,2,0:T(8,128)S(1)}, /...) while((s32[]{:T(128)}, f32[128,8]{0,1:T(8,128)S(1)}, f32[128,8]{0,1:T(8,128)S(1)}, ...), condition=%wide.region_3.4_spmd, body=%wide.region_2.3_spmd.sunk | while | flops 399362 | bytes 1630309 | solution.py:14
  97.4 0.1 copy.47
  97.5 0.1 copy.48
  97.6 1.4 fusion.26
  99.1 0.1 copy.47
  99.2 0.1 copy.48
  99.3 1.4 fusion.26
  100.7 0.1 copy.47
  100.8 0.1 copy.48
  100.9 1.4 fusion.26
  102.4 0.1 copy.47
  102.5 0.1 copy.48
  102.6 1.4 fusion.26
  104.1 0.1 copy.47
  104.2 0.1 copy.48
  104.3 1.4 fusion.26
  105.8 0.1 copy.47
  105.9 0.1 copy.48
  106.0 1.4 fusion.26
  107.5 0.1 copy.47
  107.6 0.1 copy.48
  107.7 1.4 fusion.26
  109.1 0.1 copy.22
  109.2 0.2 divide_convert_fusion
  109.4 2.5 %fusion.14 = f32[128,576]{0,1:T(8,128)} fusion(bf16[576,1024]{1,0:T(8,128)(2,1)} %param.12, bf16[16,8,8,128]{3,2,1,0:T(8,128)(2,1)S(1)} %bitcast.57), kind=kOutput, calls=%fused_computation.25 | convolution fusion | flops 150994944 | bytes 1736704 | tf_op jit(solution)/shard_map/dot_general | solution.py:59
  111.9 0.0 all-reduce.2.cloned.1.call-update
  111.9 31.2 %all-reduce.2.cloned.1.call-done = f32[128,576]{0,1:T(8,128)} async-done(((f32[128,576]{0,1:T(8,128)}), f32[128,576]{0,1:T(8,128)}) %all-reduce.2.cloned.1.call-update) | async-done | bytes 294928 | tf_op jit(solution)/shard_map/psum | solution.py:62
  143.1 1.1 multiply_reduce_fusion
  144.2 21.4 %psum.15 = f32[128]{0:T(128)S(1)} all-reduce(f32[128]{0:T(128)S(1)} %multiply_reduce_fusion), channel_id=1, replica_groups=mesh['seq'=8,'head'=4] {'seq'}, use_global_device_ids=true, to_apply=%region_6.7 | all-reduce | flops 128 | bytes 1024 | tf_op jit(solution)/shard_map/psum | solution.py:64
  165.5 0.0 copy-done.2
  165.5 1.8 %multiply_convert_fusion = bf16[128,576]{0,1:T(8,128)(2,1)} fusion(f32[128,576]{0,1:T(8,128)} %all-reduce.2.cloned.1.call-done, f32[576]{0:T(1024)S(1)} %copy-done.2, f32[128]{0:T(128)S(1)} %add_rsqrt_fusion), kind=kLoop, calls=%fused_computation.23 | loop fusion | flops 221184 | bytes 445184 | tf_op jit(solution)/shard_map/convert_element_type | solution.py:67
  (13 shorter events, 0.1 us)
Async XLA Ops:
  6.5 4.7 %copy-start = (bf16[2048,4,128]{2,1,0:T(4,128)(2,1)S(1)}, bf16[2048,4,128]{2,1,0:T(4,128)(2,1)}, u32[]{:S(2)}) copy-start(bf16[2048,4,128]{2,1,0:T(4,128)(2,1)} %param.10) | copy-start | bytes 6291460
  6.5 85.7 %all-gather.2.cloned.1.call-start = ((), (), s32[]{:S(2)}) async-start(), calls=%async_computation | async-start | bytes 4718592 | tf_op jit(solution)/shard_map/all_gather | solution.py:11
  11.2 3.5 %copy-start.1 = (f32[4,2048,128,2]{2,1,3,0:T(8,128)}, f32[4,2048,128,2]{2,1,3,0:T(8,128)S(1)}, u32[]{:S(2)}) copy-start(f32[4,2048,128,2]{2,1,3,0:T(8,128)S(1)} %get-tuple-element.64) | copy-start | bytes 25165828
  15.9 127.2 %all-reduce.2.cloned.1.call-start = ((), (), s32[]{:S(2)}) async-start(), calls=%async_computation.1 | async-start | bytes 589824 | tf_op jit(solution)/shard_map/psum | solution.py:62
  93.3 72.2 %copy-start.2 = (f32[576]{0:T(1024)S(1)}, f32[576]{0:T(1024)}, u32[]{:S(2)}) copy-start(f32[576]{0:T(1024)} %param.13) | copy-start | bytes 6916
Sparse Core Ops, SparseCore 0:
  16.0 76.1 all-gather.1
  112.0 31.0 all-reduce.1
where the time goes:
time: 175 us; the launch traced here: 174 us
  blocking collectives  86.2 us (49%)
  waiting for transfers between devices  38.1 us (22%)
  other arithmetic  17.8 us (10%)
  between operations  14.3 us (8%)
  matrix products  9.75 us (6%)
  local copies, waits for them, and re-layouts  7.82 us (4%)
    all_gather x2, blocking collectives, merged(): pieces = jax.tree.map(lambda part: lax.all_gather(part, axis), value)  64.8 us
    psum x1, waiting for transfers between devices, body(): projected = lax.psum(projected_part, 'head')  31.2 us
    psum x1, blocking collectives, body(): square_total = lax.psum(square_part, 'seq')  21.4 us
    add x7, other arithmetic, combine_partials(): factor_former[..., None] * acc_former  10 us
    all_gather x1, waiting for transfers between devices, merged(): pieces = jax.tree.map(lambda part: lax.all_gather(part, axis), value)  6.87 us
    reduce_sum x1, other arithmetic, body(): block_sum = jnp.sum(weights, axis=-1)  4.59 us
    slice x3, local copies, waits for them, and re-layouts, merged(): tail = jax.tree.map(lambda part: part[1:], pieces)  4.08 us
    dot_general x1, matrix products, body(): jnp.einsum('tkgd,ckd->kgtc', grouped, key_cache, preferred_element_type=j...  3.86 us
  transfers between devices with their start and end apart: 2, of which 2 were waited for; matrix products, arithmetic and copies ran while one was open for 3% of the time, Pallas kernels for 0%

commit v1 on v0

v1 whole, which is shorter than its diff:
```python
import functools
import math

import jax
import jax.numpy as jnp
from jax import lax
from jax.experimental import pallas as pl
from jax.experimental.pallas import tpu as pltpu
from jax.sharding import PartitionSpec as P

QPRE = 144
MESH = pl.DeviceIdType.MESH
BF16 = jnp.bfloat16
F32 = jnp.float32
NEG = -1e30


def kernel(cfg, q_hbm, k_hbm, v_hbm, len_ref, w_hbm, gain_ref, out_ref,
           qin, kin, vin, win, stage, qd, kd, vt, s_scr,
           acc_send, acc_rec, st_send, st_rec, attn, psend, prec, pg, ss_send, ss_rec,
           lsem, a_ssem, a_rsem, t_ssem, t_rsem, g_ssem, g_rsem, p_ssem, p_rsem,
           r_ssem, r_rsem, s_ssem, s_rsem):
    n, hn, keys, kvl, group, tok, hd, feat, split, blk = cfg
    heads = kvl * group
    width = heads * hd
    cr = width // n
    fq = feat // hn if split else feat
    fpad = pg.shape[0]
    me = lax.axis_index("seq")
    hm = lax.axis_index("head")
    tid = me * hn + hm
    total_dev = n * hn
    coef = float(QPRE) ** (-0.5) * math.log2(math.e)

    cq = pltpu.make_async_copy(q_hbm, qin, lsem.at[0])
    ck = pltpu.make_async_copy(k_hbm, kin, lsem.at[1])
    cv = pltpu.make_async_copy(v_hbm, vin, lsem.at[2])
    cw = pltpu.make_async_copy(w_hbm, win, lsem.at[3])
    cq.start()
    ck.start()
    cv.start()
    cw.start()

    barrier = pltpu.get_barrier_semaphore()
    if split:
        @pl.loop(1, total_dev)
        def _(d):
            t = lax.rem(tid + d, total_dev)
            pl.semaphore_signal(barrier, inc=1, device_id=(t // hn, lax.rem(t, hn)), device_id_type=MESH)
        arrivals = total_dev - 1
    else:
        @pl.loop(1, n)
        def _(d):
            pl.semaphore_signal(barrier, inc=1, device_id=(lax.rem(me + d, n), hm), device_id_type=MESH)
        for d in range(1, hn):
            pl.semaphore_signal(barrier, inc=1, device_id=(me, lax.rem(hm + d, hn)), device_id_type=MESH)
        arrivals = n + hn - 2

    cq.wait()
    stage[0:tok * heads, :] = qin[...].astype(F32)
    for h in range(heads):
        qd[h // group, (h % group) * tok:(h % group + 1) * tok, :] = (
            stage[pl.ds(h, tok, stride=heads), :].astype(BF16))
    ck.wait()

    @pl.loop(0, keys // blk)
    def _(c):
        row = pl.multiple_of(c * (blk * kvl), blk * kvl)
        col = pl.multiple_of(c * blk, blk)
        stage[0:blk * kvl, :] = kin[pl.ds(row, blk * kvl), :].astype(F32)
        for h in range(kvl):
            kd[h, pl.ds(col, blk), :] = stage[pl.ds(h, blk, stride=kvl), :].astype(BF16)

    cv.wait()

    @pl.loop(0, keys // blk)
    def _(c):
        row = pl.multiple_of(c * (blk * kvl), blk * kvl)
        col = pl.multiple_of(c * blk, blk)
        stage[0:blk * kvl, :] = vin[pl.ds(row, blk * kvl), :].astype(F32)
        for h in range(kvl):
            vt[h, :, pl.ds(col, blk)] = stage[pl.ds(h, blk, stride=kvl), :].T.astype(BF16)

    valid = len_ref[0]
    per = group * hd // cr
    rows = group * tok

    def acc_copy(dest, src):
        return pltpu.make_async_remote_copy(
            src_ref=acc_send.at[pl.ds(pl.multiple_of(dest * cr, cr), cr), :],
            dst_ref=acc_rec.at[src], send_sem=a_ssem.at[dest], recv_sem=a_rsem.at[src],
            device_id=(dest, hm), device_id_type=MESH)

    def st_copy(dest, src):
        return pltpu.make_async_remote_copy(
            src_ref=st_send.at[(dest * cr) // hd],
            dst_ref=st_rec.at[src], send_sem=t_ssem.at[dest], recv_sem=t_rsem.at[src],
            device_id=(dest, hm), device_id_type=MESH)

    first = (me * cr) // (hd * group) + 1

    @pl.loop(0, kvl)
    def _(i):
        k = lax.rem(first + i, kvl)
        qq = qd[k]
        peak8 = jnp.full((8, rows), NEG, F32)
        for c in range(0, keys, blk):
            s = lax.dot_general(kd[k, c:c + blk, :], qq, (((1,), (1,)), ((), ())),
                                preferred_element_type=F32)
            pos = lax.broadcasted_iota(jnp.int32, (blk, rows), 0) + c
            s = jnp.where(pos < valid, s, NEG)
            s_scr[c:c + blk, :] = s
            peak8 = jnp.maximum(peak8, jnp.max(s.reshape(blk // 8, 8, rows), axis=0))
        peak = jnp.max(peak8, axis=0, keepdims=True)
        sum8 = jnp.zeros((8, rows), F32)
        acc = jnp.zeros((hd, rows), F32)
        for c in range(0, keys, blk):
            w = jnp.exp2((s_scr[c:c + blk, :] - peak) * coef)
            sum8 = sum8 + jnp.sum(w.reshape(blk // 8, 8, rows), axis=0)
            acc = acc + jnp.dot(vt[k, :, c:c + blk], w.astype(BF16), preferred_element_type=F32)
        total = jnp.sum(sum8, axis=0, keepdims=True)
        low = acc.astype(BF16)
        for g in range(group):
            h = k * group + g
            acc_send[pl.ds(pl.multiple_of(h * hd, hd), hd), :] = low[:, g * tok:(g + 1) * tok]
            st_send[h, 0:1, :] = peak[:, g * tok:(g + 1) * tok]
            st_send[h, 1:2, :] = total[:, g * tok:(g + 1) * tok]

        @pl.when(i == 0)
        def _():
            pl.semaphore_wait(barrier, arrivals)

        for j in range(per):
            dest = k * per + j

            @pl.when(dest != me)
            def _():
                st_copy(dest, me).start()
                acc_copy(dest, me).start()

    acc_rec[me] = acc_send[pl.ds(pl.multiple_of(me * cr, cr), cr), :]
    st_rec[me] = st_send[(me * cr) // hd]

    @pl.loop(1, n)
    def _(d):
        src = lax.rem(me + d, n)
        st_copy(src, src).wait_recv()
        acc_copy(src, src).wait_recv()

    top = st_rec[0, 0:1, :]
    for b in range(1, n):
        top = jnp.maximum(top, st_rec[b, 0:1, :])
    whole = jnp.zeros((1, tok), F32)
    comb = jnp.zeros((cr, tok), F32)
    for b in range(n):
        f = jnp.exp2((st_rec[b, 0:1, :] - top) * coef)
        whole = whole + f * st_rec[b, 1:2, :]
        comb = comb + f * acc_rec[b].astype(F32)
    attn[pl.ds(pl.multiple_of(me * cr, cr), cr), :] = (comb / whole).astype(BF16)

    def g_copy(owner, dest):
        part = pl.ds(pl.multiple_of(owner * cr, cr), cr)
        return pltpu.make_async_remote_copy(
            src_ref=attn.at[part, :], dst_ref=attn.at[part, :],
            send_sem=g_ssem.at[dest], recv_sem=g_rsem.at[owner],
            device_id=(dest, hm), device_id_type=MESH)

    @pl.loop(1, n)
    def _(d):
        g_copy(me, lax.rem(me + d, n)).start()

    cw.wait()

    @pl.loop(1, n)
    def _(d):
        src = lax.rem(me + d, n)
        g_copy(src, src).wait_recv()

    proj = jnp.dot(win[...], attn[...], preferred_element_type=F32)
    psend[...] = proj.astype(BF16)

    def p_copy(owner, dest):
        part = psend.at[pl.ds(pl.multiple_of(dest * fq, fq), fq), :] if split else psend
        return pltpu.make_async_remote_copy(
            src_ref=part, dst_ref=prec.at[owner],
            send_sem=p_ssem.at[dest], recv_sem=p_rsem.at[owner],
            device_id=(me, dest), device_id_type=MESH)

    for d in range(1, hn):
        p_copy(hm, lax.rem(hm + d, hn)).start()
    if split:
        prec[hm] = psend[pl.ds(pl.multiple_of(hm * fq, fq), fq), :]
    else:
        prec[hm] = psend[...]
    for d in range(1, hn):
        src = lax.rem(hm + d, hn)
        p_copy(src, src).wait_recv()
    mine = prec[0].astype(F32)
    for b in range(1, hn):
        mine = mine + prec[b].astype(F32)

    def r_copy(owner, dest):
        part = pl.ds(pl.multiple_of(owner * fq, fq), fq)
        return pltpu.make_async_remote_copy(
            src_ref=pg.at[part, :], dst_ref=pg.at[part, :],
            send_sem=r_ssem.at[dest], recv_sem=r_rsem.at[owner],
            device_id=(me, dest), device_id_type=MESH)

    ss_send[...] = jnp.sum((mine * mine).reshape(fq // 8, 8, tok), axis=0)
    members = total_dev if split else n
    mid = tid if split else me

    def s_copy(owner, dest):
        to = (dest // hn, lax.rem(dest, hn)) if split else (dest, hm)
        return pltpu.make_async_remote_copy(
            src_ref=ss_send, dst_ref=ss_rec.at[owner],
            send_sem=s_ssem.at[dest], recv_sem=s_rsem.at[owner],
            device_id=to, device_id_type=MESH)

    @pl.loop(1, members)
    def _(d):
        s_copy(mid, lax.rem(mid + d, members)).start()
    ss_rec[mid] = ss_send[...]

    if fpad > feat:
        pg[feat:fpad, :] = jnp.zeros((fpad - feat, tok), BF16)
    if split:
        pg[pl.ds(pl.multiple_of(hm * fq, fq), fq), :] = mine.astype(BF16)
        for d in range(1, hn):
            r_copy(hm, lax.rem(hm + d, hn)).start()
        for d in range(1, hn):
            src = lax.rem(hm + d, hn)
            r_copy(src, src).wait_recv()
    else:
        pg[0:feat, :] = mine.astype(BF16)

    @pl.loop(1, members)
    def _(d):
        src = lax.rem(mid + d, members)
        s_copy(src, src).wait_recv()

    square = jnp.sum(jnp.sum(ss_rec[...], axis=0), axis=0, keepdims=True)
    factor = lax.rsqrt(square / (feat * n) + 1e-06)
    normed = (pg[...].astype(F32) * factor).T
    out_ref[...] = (normed[:, 0:feat] * gain_ref[...]).astype(BF16)

    @pl.loop(1, n)
    def _(d):
        dest = lax.rem(me + d, n)
        st_copy(dest, me).wait_send()
        acc_copy(dest, me).wait_send()
        g_copy(me, dest).wait_send()
    for d in range(1, hn):
        dest = lax.rem(hm + d, hn)
        p_copy(hm, dest).wait_send()
        if split:
            r_copy(hm, dest).wait_send()

    @pl.loop(1, members)
    def _(d):
        s_copy(mid, lax.rem(mid + d, members)).wait_send()


def body(n, hn, query, key_cache, value_cache, lengths, out_weight, norm_gain):
    tok, heads, hd = query.shape
    keys, kvl, _ = key_cache.shape
    feat, width = out_weight.shape
    group = heads // kvl
    split = feat % (16 * hn) == 0
    blk = 256
    cr = width // n
    fq = feat // hn if split else feat
    fpad = -(-feat // 128) * 128
    members = n * hn if split else n
    cfg = (n, hn, keys, kvl, group, tok, hd, feat, split, blk)
    dma = pltpu.SemaphoreType.DMA
    hbm = pl.BlockSpec(memory_space=pl.ANY)
    return pl.pallas_call(
        functools.partial(kernel, cfg),
        out_shape=jax.ShapeDtypeStruct((tok, feat), BF16),
        in_specs=[hbm, hbm, hbm, pl.BlockSpec(memory_space=pltpu.SMEM), hbm,
                  pl.BlockSpec(memory_space=pltpu.VMEM)],
        out_specs=pl.BlockSpec(memory_space=pltpu.VMEM),
        scratch_shapes=[
            pltpu.VMEM((tok * heads, hd), BF16),
            pltpu.VMEM((keys * kvl, hd), BF16),
            pltpu.VMEM((keys * kvl, hd), BF16),
            pltpu.VMEM((feat, width), BF16),
            pltpu.VMEM((max(blk * kvl, tok * heads), hd), F32),
            pltpu.VMEM((kvl, group * tok, hd), BF16),
            pltpu.VMEM((kvl, keys, hd), BF16),
            pltpu.VMEM((kvl, hd, keys), BF16),
            pltpu.VMEM((keys, group * tok), F32),
            pltpu.VMEM((width, tok), BF16),
            pltpu.VMEM((n, cr, tok), BF16),
            pltpu.VMEM((heads, 8, tok), F32),
            pltpu.VMEM((n, 8, tok), F32),
            pltpu.VMEM((width, tok), BF16),
            pltpu.VMEM((feat, tok), BF16),
            pltpu.VMEM((hn, fq, tok), BF16),
            pltpu.VMEM((fpad, tok), BF16),
            pltpu.VMEM((8, tok), F32),
            pltpu.VMEM((members, 8, tok), F32),
            dma((4,)), dma((n,)), dma((n,)), dma((n,)), dma((n,)), dma((n,)), dma((n,)),
            dma((hn,)), dma((hn,)), dma((hn,)), dma((hn,)), dma((members,)), dma((members,)),
        ],
        compiler_params=pltpu.CompilerParams(collective_id=0, has_side_effects=True),
    )(query.reshape(tok * heads, hd), key_cache.reshape(keys * kvl, hd),
      value_cache.reshape(keys * kvl, hd), lengths, out_weight, norm_gain.reshape(1, feat))


def solution(mesh):
    placed = (
        P(None, "head", None),
        P("seq", "head", None),
        P("seq", "head", None),
        P("seq"),
        P("seq", "head"),
        P("seq"),
    )
    return jax.shard_map(
        functools.partial(body, mesh.shape["seq"], mesh.shape["head"]),
        mesh=mesh, in_specs=placed, out_specs=P(None, "seq"), check_vma=False,
    )
```

time: 175 us -> 40.2 us (0.23)
  blocking collectives: 86.2 us -> 0 us
  waiting for transfers between devices: 38.1 us -> 0 us
  Pallas kernels: 0 us -> 36.4 us
  other arithmetic: 17.8 us -> 0 us
  between operations: 14.3 us -> 0.66 us
  matrix products: 9.75 us -> 0 us
  local copies, waits for them, and re-layouts: 7.82 us -> 2.96 us
    all_gather x2 -> x0, blocking collectives: 64.8 us -> none  [merged(): pieces = jax.tree.map(lambda part: lax.all_gather(part, axis), value)]
    pallas_call x0 -> x1, Pallas kernels: none -> 36.4 us  [body(): pl.pallas_call(functools.partial(kernel, cfg), out_shape=jax.ShapeDtypeSt...]
    psum x1 -> x0, waiting for transfers between devices: 31.2 us -> none  [body(): projected = lax.psum(projected_part, 'head')]
    psum x1 -> x0, blocking collectives: 21.4 us -> none  [body(): square_total = lax.psum(square_part, 'seq')]
    add x14 -> x0, other arithmetic: 10.2 us -> none  [the longest x7 10 us: combine_partials(): factor_former[..., None] * acc_former]
    dot_general x3 -> x0, matrix products: 9.75 us -> none  [the longest x1 3.86 us: body(): jnp.einsum('tkgd,ckd->kgtc', grouped, key_cache, preferred_element_type=j...]
    all_gather x1 -> x0, waiting for transfers between devices: 6.87 us -> none  [merged(): pieces = jax.tree.map(lambda part: lax.all_gather(part, axis), value)]
    reduce_sum x2 -> x0, other arithmetic: 5.64 us -> none  [the longest x1 4.59 us: body(): block_sum = jnp.sum(weights, axis=-1)]
  transfers between devices with their start and end apart: 2 -> 0, of which waited for: 2 -> 0; matrix products, arithmetic and copies ran while one was open for 3% -> 0% of each run, Pallas kernels for 0% -> 0%
where the time goes in v1:
time: 40.2 us; the launch traced here: 40 us
  Pallas kernels  36.4 us (91%)
  local copies, waits for them, and re-layouts  2.96 us (7%)
  between operations  0.66 us (2%)
    pallas_call x1, Pallas kernels, body(): pl.pallas_call(functools.partial(kernel, cfg), out_shape=jax.ShapeDtypeSt...  36.4 us
    pallas_call x1, local copies, waits for them, and re-layouts, body(): pl.pallas_call(functools.partial(kernel, cfg), out_shape=jax.ShapeDtypeSt...  1.7 us
    reshape x1, local copies, waits for them, and re-layouts, body(): norm_gain.reshape(1, feat)  1.27 us

profile of v1, /device:TPU:0, one launch (start us, length us, event | category | flops | bytes accessed | tf_op | source)
XLA Modules:
  0.0 40.0 jit_solution(16150754543853915646)
XLA Ops:
  0.7 1.3 %reshape.15.gain_ref = f32[1,576]{1,0:T(1,128)} reshape(f32[576]{0:T(1024)} %param.11) | data formatting | bytes 4608 | tf_op jit(solution)/shard_map/reshape | solution.py:309
  1.9 36.4 %shard_map.64 = bf16[128,576]{1,0:T(8,128)(2,1)} custom-call(bf16[1024,128]{1,0:T(8,128)(2,1)} %bitcast.5, bf16[8192,128]{1,0:T(8,128)(2,1)} %bitcast.3, bf16[8192,128]{1,0:T(8,128)(2,1)} %bitcast.4, s32[1]{0:T(128)S(6)} %copy.8.len_ref, bf16[576,1024]{1,0:T(8,128)(2,1)} %w_hbm.1, f32[1,576]{1,0:T(1,128)} %reshape.15.gain_ref), custom_call_target="tpu_custom_call" | custom-call | tf_op jit(solution)/shard_map/pallas_call | solution.py:278
  38.3 1.7 %copy.7 = bf16[128,576]{0,1:T(8,128)(2,1)} copy(bf16[128,576]{1,0:T(8,128)(2,1)} %shard_map.64) | data formatting | bytes 294912 | tf_op jit(solution)/shard_map/pallas_call | solution.py:278

commit v2 on v1

--- a/solution.py
+++ b/solution.py
@@ -15,17 +15,16 @@
 NEG = -1e30
 
 
-def kernel(cfg, q_hbm, k_hbm, v_hbm, len_ref, w_hbm, gain_ref, out_ref,
-           qin, kin, vin, win, stage, qd, kd, vt, s_scr,
+def kernel(cfg, q_hbm, k_hbm, v_hbm, len_ref, w_hbm, out_ref,
+           qin, kin, vin, win, stage, qd, kd, vd, s_scr,
            acc_send, acc_rec, st_send, st_rec, attn, psend, prec, pg, ss_send, ss_rec,
-           lsem, a_ssem, a_rsem, t_ssem, t_rsem, g_ssem, g_rsem, p_ssem, p_rsem,
+           lsem, k_sem, v_sem, a_ssem, a_rsem, t_ssem, t_rsem, g_ssem, g_rsem, f_ssem, p_ssem, p_rsem,
            r_ssem, r_rsem, s_ssem, s_rsem):
     n, hn, keys, kvl, group, tok, hd, feat, split, blk = cfg
     heads = kvl * group
     width = heads * hd
     cr = width // n
     fq = feat // hn if split else feat
-    fpad = pg.shape[0]
     me = lax.axis_index("seq")
     hm = lax.axis_index("head")
     tid = me * hn + hm
@@ -33,12 +32,17 @@
     coef = float(QPRE) ** (-0.5) * math.log2(math.e)
 
     cq = pltpu.make_async_copy(q_hbm, qin, lsem.at[0])
-    ck = pltpu.make_async_copy(k_hbm, kin, lsem.at[1])
-    cv = pltpu.make_async_copy(v_hbm, vin, lsem.at[2])
-    cw = pltpu.make_async_copy(w_hbm, win, lsem.at[3])
+    cw = pltpu.make_async_copy(w_hbm, win, lsem.at[1])
+
+    def cache_copy(src, dst, sem, c):
+        part = pl.ds(pl.multiple_of(c * (blk * kvl), blk * kvl), blk * kvl)
+        return pltpu.make_async_copy(src.at[part, :], dst.at[part, :], sem.at[c])
+
     cq.start()
-    ck.start()
-    cv.start()
+    for c in range(keys // blk):
+        cache_copy(k_hbm, kin, k_sem, c).start()
+    for c in range(keys // blk):
+        cache_copy(v_hbm, vin, v_sem, c).start()
     cw.start()
 
     barrier = pltpu.get_barrier_semaphore()
@@ -61,25 +65,16 @@
     for h in range(heads):
         qd[h // group, (h % group) * tok:(h % group + 1) * tok, :] = (
             stage[pl.ds(h, tok, stride=heads), :].astype(BF16))
-    ck.wait()
-
-    @pl.loop(0, keys // blk)
-    def _(c):
-        row = pl.multiple_of(c * (blk * kvl), blk * kvl)
-        col = pl.multiple_of(c * blk, blk)
-        stage[0:blk * kvl, :] = kin[pl.ds(row, blk * kvl), :].astype(F32)
-        for h in range(kvl):
-            kd[h, pl.ds(col, blk), :] = stage[pl.ds(h, blk, stride=kvl), :].astype(BF16)
-
-    cv.wait()
-
-    @pl.loop(0, keys // blk)
-    def _(c):
-        row = pl.multiple_of(c * (blk * kvl), blk * kvl)
-        col = pl.multiple_of(c * blk, blk)
-        stage[0:blk * kvl, :] = vin[pl.ds(row, blk * kvl), :].astype(F32)
-        for h in range(kvl):
-            vt[h, :, pl.ds(col, blk)] = stage[pl.ds(h, blk, stride=kvl), :].T.astype(BF16)
+
+    for held, src, split_ref, sem in ((kin, k_hbm, kd, k_sem), (vin, v_hbm, vd, v_sem)):
+        @pl.loop(0, keys // blk)
+        def _(c):
+            row = pl.multiple_of(c * (blk * kvl), blk * kvl)
+            col = pl.multiple_of(c * blk, blk)
+            cache_copy(src, held, sem, c).wait()
+            stage[0:blk * kvl, :] = held[pl.ds(row, blk * kvl), :].astype(F32)
+            for h in range(kvl):
+                split_ref[h, pl.ds(col, blk), :] = stage[pl.ds(h, blk, stride=kvl), :].astype(BF16)
 
     valid = len_ref[0]
     per = group * hd // cr
@@ -103,28 +98,31 @@
     def _(i):
         k = lax.rem(first + i, kvl)
         qq = qd[k]
-        peak8 = jnp.full((8, rows), NEG, F32)
+        peaks = jnp.full((rows, 128), NEG, F32)
         for c in range(0, keys, blk):
-            s = lax.dot_general(kd[k, c:c + blk, :], qq, (((1,), (1,)), ((), ())),
+            s = lax.dot_general(qq, kd[k, c:c + blk, :], (((1,), (1,)), ((), ())),
                                 preferred_element_type=F32)
-            pos = lax.broadcasted_iota(jnp.int32, (blk, rows), 0) + c
-            s = jnp.where(pos < valid, s, NEG)
-            s_scr[c:c + blk, :] = s
-            peak8 = jnp.maximum(peak8, jnp.max(s.reshape(blk // 8, 8, rows), axis=0))
-        peak = jnp.max(peak8, axis=0, keepdims=True)
-        sum8 = jnp.zeros((8, rows), F32)
-        acc = jnp.zeros((hd, rows), F32)
+            pos = lax.broadcasted_iota(jnp.int32, (1, blk), 1) + c
+            s = s + jnp.where(pos < valid, 0.0, NEG)
+            s_scr[:, c:c + blk] = s
+            for j in range(0, blk, 128):
+                peaks = jnp.maximum(peaks, s[:, j:j + 128])
+        peak = jnp.max(peaks, axis=1, keepdims=True)
+        sums = jnp.zeros((rows, 128), F32)
+        acc = jnp.zeros((rows, hd), F32)
         for c in range(0, keys, blk):
-            w = jnp.exp2((s_scr[c:c + blk, :] - peak) * coef)
-            sum8 = sum8 + jnp.sum(w.reshape(blk // 8, 8, rows), axis=0)
-            acc = acc + jnp.dot(vt[k, :, c:c + blk], w.astype(BF16), preferred_element_type=F32)
-        total = jnp.sum(sum8, axis=0, keepdims=True)
-        low = acc.astype(BF16)
+            w = jnp.exp2((s_scr[:, c:c + blk] - peak) * coef)
+            for j in range(0, blk, 128):
+                sums = sums + w[:, j:j + 128]
+            acc = acc + jnp.dot(w.astype(BF16), vd[k, c:c + blk, :], preferred_element_type=F32)
+        total = jnp.sum(sums, axis=1, keepdims=True)
+        lane = lax.broadcasted_iota(jnp.int32, (rows, 128), 1)
+        stats = jnp.where(lane == 0, peak, total).T
+        low = acc.T.astype(BF16)
         for g in range(group):
             h = k * group + g
             acc_send[pl.ds(pl.multiple_of(h * hd, hd), hd), :] = low[:, g * tok:(g + 1) * tok]
-            st_send[h, 0:1, :] = peak[:, g * tok:(g + 1) * tok]
-            st_send[h, 1:2, :] = total[:, g * tok:(g + 1) * tok]
+            st_send[h] = stats[0:8, g * tok:(g + 1) * tok]
 
         @pl.when(i == 0)
         def _():
@@ -165,15 +163,33 @@
             send_sem=g_ssem.at[dest], recv_sem=g_rsem.at[owner],
             device_id=(dest, hm), device_id_type=MESH)
 
-    @pl.loop(1, n)
-    def _(d):
-        g_copy(me, lax.rem(me + d, n)).start()
+    side = lax.rem(me, 2)
+    partner = me + 1 - 2 * side
+
+    def f_copy(owner):
+        part = pl.ds(pl.multiple_of(owner * cr, cr), cr)
+        return pltpu.make_async_remote_copy(
+            src_ref=attn.at[part, :], dst_ref=attn.at[part, :],
+            send_sem=f_ssem.at[owner], recv_sem=g_rsem.at[owner],
+            device_id=(partner, hm), device_id_type=MESH)
+
+    @pl.loop(1, n // 2)
+    def _(d):
+        g_copy(me, lax.rem(me + 2 * d, n)).start()
+    g_copy(me, partner).start()
 
     cw.wait()
 
-    @pl.loop(1, n)
-    def _(d):
-        src = lax.rem(me + d, n)
+    @pl.loop(1, n // 2)
+    def _(d):
+        src = lax.rem(me + 2 * d, n)
+        g_copy(src, src).wait_recv()
+        f_copy(src).start()
+    g_copy(partner, partner).wait_recv()
+
+    @pl.loop(1, n // 2)
+    def _(d):
+        src = lax.rem(partner + 2 * d, n)
         g_copy(src, src).wait_recv()
 
     proj = jnp.dot(win[...], attn[...], preferred_element_type=F32)
@@ -222,8 +238,6 @@
         s_copy(mid, lax.rem(mid + d, members)).start()
     ss_rec[mid] = ss_send[...]
 
-    if fpad > feat:
-        pg[feat:fpad, :] = jnp.zeros((fpad - feat, tok), BF16)
     if split:
         pg[pl.ds(pl.multiple_of(hm * fq, fq), fq), :] = mine.astype(BF16)
         for d in range(1, hn):
@@ -232,7 +246,7 @@
             src = lax.rem(hm + d, hn)
             r_copy(src, src).wait_recv()
     else:
-        pg[0:feat, :] = mine.astype(BF16)
+        pg[...] = mine.astype(BF16)
 
     @pl.loop(1, members)
     def _(d):
@@ -241,15 +255,20 @@
 
     square = jnp.sum(jnp.sum(ss_rec[...], axis=0), axis=0, keepdims=True)
     factor = lax.rsqrt(square / (feat * n) + 1e-06)
-    normed = (pg[...].astype(F32) * factor).T
-    out_ref[...] = (normed[:, 0:feat] * gain_ref[...]).astype(BF16)
+    out_ref[...] = pg[...].astype(F32) * factor
 
     @pl.loop(1, n)
     def _(d):
         dest = lax.rem(me + d, n)
         st_copy(dest, me).wait_send()
         acc_copy(dest, me).wait_send()
+
+    @pl.loop(1, n // 2)
+    def _(d):
+        dest = lax.rem(me + 2 * d, n)
         g_copy(me, dest).wait_send()
+        f_copy(dest).wait_send()
+    g_copy(me, partner).wait_send()
     for d in range(1, hn):
         dest = lax.rem(hm + d, hn)
         p_copy(hm, dest).wait_send()
@@ -267,19 +286,17 @@
     feat, width = out_weight.shape
     group = heads // kvl
     split = feat % (16 * hn) == 0
-    blk = 256
+    blk = math.gcd(keys, 512)
     cr = width // n
     fq = feat // hn if split else feat
-    fpad = -(-feat // 128) * 128
     members = n * hn if split else n
     cfg = (n, hn, keys, kvl, group, tok, hd, feat, split, blk)
     dma = pltpu.SemaphoreType.DMA
     hbm = pl.BlockSpec(memory_space=pl.ANY)
-    return pl.pallas_call(
+    scaled = pl.pallas_call(
         functools.partial(kernel, cfg),
-        out_shape=jax.ShapeDtypeStruct((tok, feat), BF16),
-        in_specs=[hbm, hbm, hbm, pl.BlockSpec(memory_space=pltpu.SMEM), hbm,
-                  pl.BlockSpec(memory_space=pltpu.VMEM)],
+        out_shape=jax.ShapeDtypeStruct((feat, tok), F32),
+        in_specs=[hbm, hbm, hbm, pl.BlockSpec(memory_space=pltpu.SMEM), hbm],
         out_specs=pl.BlockSpec(memory_space=pltpu.VMEM),
         scratch_shapes=[
             pltpu.VMEM((tok * heads, hd), BF16),
@@ -289,8 +306,8 @@
             pltpu.VMEM((max(blk * kvl, tok * heads), hd), F32),
             pltpu.VMEM((kvl, group * tok, hd), BF16),
             pltpu.VMEM((kvl, keys, hd), BF16),
-            pltpu.VMEM((kvl, hd, keys), BF16),
-            pltpu.VMEM((keys, group * tok), F32),
+            pltpu.VMEM((kvl, keys, hd), BF16),
+            pltpu.VMEM((group * tok, keys), F32),
             pltpu.VMEM((width, tok), BF16),
             pltpu.VMEM((n, cr, tok), BF16),
             pltpu.VMEM((heads, 8, tok), F32),
@@ -298,15 +315,16 @@
             pltpu.VMEM((width, tok), BF16),
             pltpu.VMEM((feat, tok), BF16),
             pltpu.VMEM((hn, fq, tok), BF16),
-            pltpu.VMEM((fpad, tok), BF16),
+            pltpu.VMEM((feat, tok), BF16),
             pltpu.VMEM((8, tok), F32),
             pltpu.VMEM((members, 8, tok), F32),
-            dma((4,)), dma((n,)), dma((n,)), dma((n,)), dma((n,)), dma((n,)), dma((n,)),
-            dma((hn,)), dma((hn,)), dma((hn,)), dma((hn,)), dma((members,)), dma((members,)),
+            dma((2,)), dma((keys // blk,)), dma((keys // blk,)), dma((n,)), dma((n,)), dma((n,)), dma((n,)), dma((n,)), dma((n,)),
+            dma((n,)), dma((hn,)), dma((hn,)), dma((hn,)), dma((hn,)), dma((members,)), dma((members,)),
         ],
         compiler_params=pltpu.CompilerParams(collective_id=0, has_side_effects=True),
     )(query.reshape(tok * heads, hd), key_cache.reshape(keys * kvl, hd),
-      value_cache.reshape(keys * kvl, hd), lengths, out_weight, norm_gain.reshape(1, feat))
+      value_cache.reshape(keys * kvl, hd), lengths, out_weight)
+    return (scaled * norm_gain[:, None]).astype(BF16).T
 
 
 def solution(mesh):

time: 40.2 us -> 37.1 us (0.923)
  local copies, waits for them, and re-layouts: 2.96 us -> 0.01 us
  Pallas kernels: 36.4 us -> 34.5 us
  other arithmetic: 0 us -> 1.77 us
    pallas_call x1, Pallas kernels: 36.4 us -> 34.5 us  [body(): pl.pallas_call(functools.partial(kernel, cfg), out_shape=jax.ShapeDtypeSt...]
    transpose x0 -> x1, other arithmetic: none -> 1.77 us  [body(): return (scaled * norm_gain[:, None]).astype(BF16).T]
    pallas_call x1 -> x0, local copies, waits for them, and re-layouts: 1.7 us -> none  [body(): pl.pallas_call(functools.partial(kernel, cfg), out_shape=jax.ShapeDtypeSt...]
    reshape x1 -> x0, local copies, waits for them, and re-layouts: 1.27 us -> none  [body(): norm_gain.reshape(1, feat)]
where the time goes in v2:
time: 37.1 us; the launch traced here: 37 us
  Pallas kernels  34.5 us (93%)
  other arithmetic  1.77 us (5%)
  between operations  0.68 us (2%)
    pallas_call x1, Pallas kernels, body(): pl.pallas_call(functools.partial(kernel, cfg), out_shape=jax.ShapeDtypeSt...  34.5 us
    transpose x1, other arithmetic, body(): return (scaled * norm_gain[:, None]).astype(BF16).T  1.77 us

profile of v2, /device:TPU:0, one launch (start us, length us, event | category | flops | bytes accessed | tf_op | source)
XLA Modules:
  0.0 37.0 jit_solution(15630151124246216836)
XLA Ops:
  0.7 0.0 copy-start
  0.7 34.5 %shard_map.64 = f32[576,128]{1,0:T(8,128)} custom-call(bf16[1024,128]{1,0:T(8,128)(2,1)} %bitcast.7, bf16[8192,128]{1,0:T(8,128)(2,1)} %bitcast.5, bf16[8192,128]{1,0:T(8,128)(2,1)} %bitcast.6, s32[1]{0:T(128)S(6)} %copy.7.len_ref, bf16[576,1024]{1,0:T(8,128)(2,1)} %w_hbm.1), custom_call_target="tpu_custom_call" | custom-call | tf_op jit(solution)/shard_map/pallas_call | solution.py:296
  35.2 0.0 copy-done
  35.2 1.8 %fusion = bf16[128,576]{0,1:T(8,128)(2,1)} fusion(f32[576,128]{1,0:T(8,128)} %shard_map.64, f32[576]{0:T(1024)S(1)} %copy-done), kind=kLoop, calls=%fused_computation.1 | loop fusion | flops 147456 | bytes 444672 | tf_op jit(solution)/shard_map/transpose | solution.py:327
Async XLA Ops:
  0.7 34.5 %copy-start = (f32[576]{0:T(1024)S(1)}, f32[576]{0:T(1024)}, u32[]{:S(2)}) copy-start(f32[576]{0:T(1024)} %param.11) | copy-start | bytes 6916

commit v3 on v2

--- a/solution.py
+++ b/solution.py
@@ -122,7 +122,7 @@
         for g in range(group):
             h = k * group + g
             acc_send[pl.ds(pl.multiple_of(h * hd, hd), hd), :] = low[:, g * tok:(g + 1) * tok]
-            st_send[h] = stats[0:8, g * tok:(g + 1) * tok]
+            st_send[h] = stats[0:2, g * tok:(g + 1) * tok]
 
         @pl.when(i == 0)
         def _():
@@ -165,6 +165,10 @@
 
     side = lax.rem(me, 2)
     partner = me + 1 - 2 * side
+    turn = 1 - 2 * ((2 * me) // n)
+
+    def peer(d):
+        return lax.rem(me + 2 * d * turn + n, n)
 
     def f_copy(owner):
         part = pl.ds(pl.multiple_of(owner * cr, cr), cr)
@@ -175,14 +179,14 @@
 
     @pl.loop(1, n // 2)
     def _(d):
-        g_copy(me, lax.rem(me + 2 * d, n)).start()
+        g_copy(me, peer(n // 2 - d)).start()
     g_copy(me, partner).start()
 
     cw.wait()
 
     @pl.loop(1, n // 2)
     def _(d):
-        src = lax.rem(me + 2 * d, n)
+        src = peer(d)
         g_copy(src, src).wait_recv()
         f_copy(src).start()
     g_copy(partner, partner).wait_recv()
@@ -222,7 +226,7 @@
             send_sem=r_ssem.at[dest], recv_sem=r_rsem.at[owner],
             device_id=(me, dest), device_id_type=MESH)
 
-    ss_send[...] = jnp.sum((mine * mine).reshape(fq // 8, 8, tok), axis=0)
+    ss_send[...] = jnp.sum(mine * mine, axis=0, keepdims=True)
     members = total_dev if split else n
     mid = tid if split else me
 
@@ -253,7 +257,7 @@
         src = lax.rem(mid + d, members)
         s_copy(src, src).wait_recv()
 
-    square = jnp.sum(jnp.sum(ss_rec[...], axis=0), axis=0, keepdims=True)
+    square = jnp.sum(ss_rec[...], axis=0)
     factor = lax.rsqrt(square / (feat * n) + 1e-06)
     out_ref[...] = pg[...].astype(F32) * factor
 
@@ -310,14 +314,14 @@
             pltpu.VMEM((group * tok, keys), F32),
             pltpu.VMEM((width, tok), BF16),
             pltpu.VMEM((n, cr, tok), BF16),
-            pltpu.VMEM((heads, 8, tok), F32),
-            pltpu.VMEM((n, 8, tok), F32),
+            pltpu.VMEM((heads, 2, tok), F32),
+            pltpu.VMEM((n, 2, tok), F32),
             pltpu.VMEM((width, tok), BF16),
             pltpu.VMEM((feat, tok), BF16),
             pltpu.VMEM((hn, fq, tok), BF16),
             pltpu.VMEM((feat, tok), BF16),
-            pltpu.VMEM((8, tok), F32),
-            pltpu.VMEM((members, 8, tok), F32),
+            pltpu.VMEM((1, tok), F32),
+            pltpu.VMEM((members, 1, tok), F32),
             dma((2,)), dma((keys // blk,)), dma((keys // blk,)), dma((n,)), dma((n,)), dma((n,)), dma((n,)), dma((n,)), dma((n,)),
             dma((n,)), dma((hn,)), dma((hn,)), dma((hn,)), dma((hn,)), dma((members,)), dma((members,)),
         ],

time: 37.1 us -> 35.9 us (0.968)
  Pallas kernels: 34.5 us -> 33.3 us
    pallas_call x1, Pallas kernels: 34.5 us -> 33.3 us  [body(): pl.pallas_call(functools.partial(kernel, cfg), out_shape=jax.ShapeDtypeSt...]
where the time goes in v3:
time: 35.9 us; the launch traced here: 35.8 us
  Pallas kernels  33.3 us (93%)
  other arithmetic  1.77 us (5%)
  between operations  0.68 us (2%)
    pallas_call x1, Pallas kernels, body(): pl.pallas_call(functools.partial(kernel, cfg), out_shape=jax.ShapeDtypeSt...  33.3 us
    transpose x1, other arithmetic, body(): return (scaled * norm_gain[:, None]).astype(BF16).T  1.77 us

profile of v3, /device:TPU:0, one launch (start us, length us, event | category | flops | bytes accessed | tf_op | source)
XLA Modules:
  0.0 35.8 jit_solution(4623459872746439962)
XLA Ops:
  0.7 0.0 copy-start
  0.7 33.3 %shard_map.64 = f32[576,128]{1,0:T(8,128)} custom-call(bf16[1024,128]{1,0:T(8,128)(2,1)} %bitcast.7, bf16[8192,128]{1,0:T(8,128)(2,1)} %bitcast.5, bf16[8192,128]{1,0:T(8,128)(2,1)} %bitcast.6, s32[1]{0:T(128)S(6)} %copy.7.len_ref, bf16[576,1024]{1,0:T(8,128)(2,1)} %w_hbm.1), custom_call_target="tpu_custom_call" | custom-call | tf_op jit(solution)/shard_map/pallas_call | solution.py:300
  34.0 0.0 copy-done
  34.0 1.8 %fusion = bf16[128,576]{0,1:T(8,128)(2,1)} fusion(f32[576,128]{1,0:T(8,128)} %shard_map.64, f32[576]{0:T(1024)S(1)} %copy-done), kind=kLoop, calls=%fused_computation.1 | loop fusion | flops 147456 | bytes 444672 | tf_op jit(solution)/shard_map/transpose | solution.py:331
Async XLA Ops:
  0.7 33.4 %copy-start = (f32[576]{0:T(1024)S(1)}, f32[576]{0:T(1024)}, u32[]{:S(2)}) copy-start(f32[576]{0:T(1024)} %param.11) | copy-start | bytes 6916

commit v4 on v3

--- a/solution.py
+++ b/solution.py
@@ -67,7 +67,7 @@
             stage[pl.ds(h, tok, stride=heads), :].astype(BF16))
 
     for held, src, split_ref, sem in ((kin, k_hbm, kd, k_sem), (vin, v_hbm, vd, v_sem)):
-        @pl.loop(0, keys // blk)
+        @pl.loop(0, keys // blk, unroll=True)
         def _(c):
             row = pl.multiple_of(c * (blk * kvl), blk * kvl)
             col = pl.multiple_of(c * blk, blk)
@@ -94,7 +94,7 @@
 
     first = (me * cr) // (hd * group) + 1
 
-    @pl.loop(0, kvl)
+    @pl.loop(0, kvl, unroll=True)
     def _(i):
         k = lax.rem(first + i, kvl)
         qq = qd[k]

time: 35.9 us -> 35.9 us (level)
  no operation moved by 1% of the time
where the time goes in v4:
time: 35.9 us; the launch traced here: 35.8 us
  Pallas kernels  33.3 us (93%)
  other arithmetic  1.77 us (5%)
  between operations  0.68 us (2%)
    pallas_call x1, Pallas kernels, body(): pl.pallas_call(functools.partial(kernel, cfg), out_shape=jax.ShapeDtypeSt...  33.3 us
    transpose x1, other arithmetic, body(): return (scaled * norm_gain[:, None]).astype(BF16).T  1.77 us

profile of v4, /device:TPU:0, one launch (start us, length us, event | category | flops | bytes accessed | tf_op | source)
XLA Modules:
  0.0 35.8 jit_solution(1024692201167454607)
XLA Ops:
  0.7 0.0 copy-start
  0.7 33.3 %shard_map.64 = f32[576,128]{1,0:T(8,128)} custom-call(bf16[1024,128]{1,0:T(8,128)(2,1)} %bitcast.7, bf16[8192,128]{1,0:T(8,128)(2,1)} %bitcast.5, bf16[8192,128]{1,0:T(8,128)(2,1)} %bitcast.6, s32[1]{0:T(128)S(6)} %copy.7.len_ref, bf16[576,1024]{1,0:T(8,128)(2,1)} %w_hbm.1), custom_call_target="tpu_custom_call" | custom-call | tf_op jit(solution)/shard_map/pallas_call | solution.py:300
  34.0 0.0 copy-done
  34.0 1.8 %fusion = bf16[128,576]{0,1:T(8,128)(2,1)} fusion(f32[576,128]{1,0:T(8,128)} %shard_map.64, f32[576]{0:T(1024)S(1)} %copy-done), kind=kLoop, calls=%fused_computation.1 | loop fusion | flops 147456 | bytes 444672 | tf_op jit(solution)/shard_map/transpose | solution.py:331
Async XLA Ops:
  0.7 33.3 %copy-start = (f32[576]{0:T(1024)S(1)}, f32[576]{0:T(1024)}, u32[]{:S(2)}) copy-start(f32[576]{0:T(1024)} %param.11) | copy-start | bytes 6916
